TPU v7x, 32 devices: a whole 2x2x4 slice. The times are simulated.
32 devices in a mesh: groups: 2 (over y), col: 16 (over z, x, core).
Axes of the slice: x: 2, y: 2, z: 4, core: 2. Of those that a mesh axis runs over, the one named last changes fastest.
Arguments:
- fields: bfloat16 [32, 137, 2048], P(('groups', 'col')), parts along dimension 0, may hold values from -6 to 6
- level_count: int32 [2048], replicated, may hold values from 68 to 137
- owner: int32 [16], replicated, may hold values from 0 to 15, as said below
- band_start: int32 [16, 37], replicated, may hold values from 0 to 133
- interp_weights: float32 [16, 37, 4], replicated, may hold values from -3 to 3
Outputs:
- timemajor: bfloat16 [32, 37, 2048], P(('groups', 'col')), parts along dimension 0
- series: bfloat16 [96, 37, 16, 128], P(('groups', 'col')), parts along dimension 0
There are 2 independent parts, one for each index of `groups`. A program takes and returns all parts, laid end to end along the dimension named above; an argument that names none is the same for every part. Nothing has to cross between parts.
Inputs may be any that keep to these rules, and one draw needn't show every extreme that they name: No owner holds more than 3 blocks, and some owner holds exactly 3.
All inputs are finite; a program needn't handle non-finite values.
Results may differ from a plain program's by a relative error of at most 0.0085.
Values may be sent and summed in bfloat16 or wider, within the bound.
A program may use at most 64 MiB of HBM per device.

v0:
```python
import jax
import jax.numpy as jnp
from jax import lax
from jax.sharding import PartitionSpec as P

LEV = 137
PLEV = 37
BAND = 4
CBLK = 128
MOST = 3


def slot_tables(owner, devices):
    blocks = owner.shape[0]
    onehot = (owner[:, None] == jnp.arange(devices, dtype=jnp.int32)[None, :]).astype(jnp.int32)
    before = jnp.cumsum(onehot, axis=0) - onehot
    slot = jnp.sum(before * onehot, axis=1)
    global_slot = owner * MOST + slot
    hit = global_slot[:, None] == jnp.arange(devices * MOST, dtype=jnp.int32)[None, :]
    block_of = jnp.sum(jnp.where(hit, jnp.arange(blocks, dtype=jnp.int32)[:, None], 0), axis=0)
    occupied = jnp.any(hit, axis=0)
    return (global_slot, block_of, occupied)


def fill_levels(data, counts):
    lev = jnp.arange(LEV, dtype=jnp.int32)[None, :, None, None]
    wanted = counts[None, None, :, :]
    last = jnp.sum(
        jnp.where(lev == wanted - 1, data.astype(jnp.float32), 0.0), axis=1, keepdims=True
    )
    return jnp.where(lev < wanted, data, last.astype(jnp.bfloat16))


def level_matrices(weights, starts):
    lev = jnp.arange(LEV, dtype=jnp.int32)
    offsets = jnp.arange(BAND, dtype=jnp.int32)
    hit = lev[None, None, None, :] == (starts[:, :, None] + offsets[None, None, :])[:, :, :, None]
    return jnp.sum(weights[:, :, :, None] * hit.astype(jnp.float32), axis=2).astype(jnp.bfloat16)


def pack_slots(data, block_of, occupied, devices):
    taken = jnp.take(data, block_of, axis=2)
    taken = jnp.where(occupied[None, None, :, None], taken, jnp.zeros((), data.dtype))
    return taken.reshape(data.shape[0], data.shape[1], devices, MOST, data.shape[3])


def per_device(fields, level_count, owner, band_start, interp_weights):
    devices = lax.axis_size("col")
    blocks = owner.shape[0]
    steps_here = fields.shape[0]
    global_slot, block_of, occupied = slot_tables(owner, devices)
    grouped = fields.reshape(steps_here, LEV, blocks, CBLK)
    counts = level_count.reshape(blocks, CBLK)
    filled = fill_levels(grouped, counts)
    matrices = level_matrices(interp_weights, band_start)
    result = jnp.einsum(
        "bpl,tlbc->tpbc", matrices, filled, preferred_element_type=jnp.float32
    ).astype(jnp.bfloat16)
    timemajor = result.reshape(steps_here, PLEV, blocks * CBLK)
    packed = pack_slots(result, block_of, occupied, devices)
    arrived = lax.all_to_all(packed, "col", split_axis=2, concat_axis=0, tiled=True)
    arrived = arrived.reshape(devices * steps_here, PLEV, MOST, CBLK)
    series = jnp.transpose(arrived, (2, 1, 0, 3))
    return (timemajor, series)


def solution(mesh):
    placed = (P(("groups", "col"), None, None), P(), P(), P(), P())
    return jax.shard_map(
        per_device,
        mesh=mesh,
        in_specs=placed,
        out_specs=(P(("groups", "col"), None, None), P(("groups", "col"), None, None, None)),
        check_vma=False,
    )
```

profile of v0, /device:TPU:0, one launch (start us, length us, event | category | flops | bytes accessed | tf_op | source)
XLA Modules:
  0.0 30.6 jit_solution(929078646718068215)
XLA Ops:
  0.6 0.7 %fusion.7 = s32[16,16]{1,0:T(8,128)S(1)} fusion(s32[16]{0:T(128)} %param.7), kind=kLoop, calls=%fused_computation.20 | loop fusion | flops 512 | bytes 1088 | tf_op jit(solution)/shard_map/convert_element_type | solution.py:15
  1.4 0.8 %select_reduce_fusion.3 = s32[16]{0:T(128)S(1)} fusion(s32[16,16]{1,0:T(8,128)S(1)} %reduce_window_sum.11, s32[16]{0:T(128)} %param.7), kind=kLoop, calls=%fused_computation.18 | loop fusion | flops 1264 | bytes 1152 | tf_op jit(solution)/shard_map/reduce_sum | solution.py:17
  2.2 0.7 %multiply_add_fusion = s32[16]{0:T(128)S(1)} fusion(s32[16]{0:T(128)S(1)} %select_reduce_fusion.3, s32[16]{0:T(128)} %param.7), kind=kLoop, calls=%fused_computation.27 | loop fusion | flops 32 | bytes 192 | tf_op jit(solution)/shard_map/add | solution.py:18
  2.9 0.1 select_reduce_fusion.2
  3.0 0.1 reduce_sum.44
  3.1 0.1 fusion.6
  3.2 1.2 %copy.30 = bf16[18,8,16,128]{3,2,1,0:T(8,128)(2,1)S(1)} copy(bf16[18,8,16,128]{3,1,2,0:T(8,128)(2,1)} %bitcast.31) | data formatting | bytes 1179648
  4.4 0.0 copy-start.1
  4.4 0.0 copy-start.2
  4.4 0.0 copy-start.3
  4.4 0.0 copy-start
  4.4 0.1 slice.2
  4.5 0.6 %copy-done.1 = f32[16,37,4]{1,2,0:T(4,128)S(1)} copy-done((f32[16,37,4]{1,2,0:T(4,128)S(1)}, f32[16,37,4]{1,2,0:T(4,128)}, u32[]{:S(2)}) %copy-start.1) | copy-done | bytes 9496
  5.1 0.1 copy.25
  5.2 0.0 copy-done.2
  5.2 0.1 copy.24
  5.3 0.0 copy-done.3
  5.4 0.1 copy-done
  5.5 0.2 select_reduce_fusion.1
  5.7 0.1 broadcast_in_dim.63
  5.8 0.9 %select_reduce_fusion = bf16[16,37,137]{2,0,1:T(8,128)(2,1)S(1)} fusion(f32[16,37,4]{0,2,1:T(4,128)S(1)} %copy.25, s32[16,37,4]{0,2,1:T(4,128)S(1)} %iota_add_fusion), kind=kLoop, calls=%fused_computation.1 | loop fusion | flops 892144 | bytes 181152 | tf_op jit(solution)/shard_map/reduce_sum | solution.py:38
  6.7 0.3 %convolution_convert_fusion = bf16[16,128,37]{1,2,0:T(8,128)(2,1)S(1)} fusion(bf16[137,16,128]{2,1,0:T(8,128)(2,1)S(1)} %slice.2, s32[16,128]{1,0:T(8,128)S(1)} %bitcast.37, bf16[16,37,137]{2,0,1:T(8,128)(2,1)S(1)} %select_reduce_fusion, bf16[16,128]{1,0:T(8,128)(2,1)S(1)} %bitcast.38), kind=kOutput, calls=%fused_computation.7 | convolution fusion | flops 21399552 | bytes 887200 | tf_op jit(solution)/shard_map/bpl,tlbc->tpbc/dot_general | solution.py:56
  7.0 0.7 %gather_fusion = bf16[48,37,128]{2,1,0:T(8,128)(2,1)S(1)} fusion(bf16[37,16,128]{2,0,1:T(8,128)(2,1)S(1)} %bitcast.32, s32[1024]{0:T(1024)S(1)} %pad_clamp_fusion), kind=kCustom, calls=%fused_computation | custom fusion | bytes 909504 | tf_op jit(solution)/shard_map/jit(_take)/gather | solution.py:42
  7.7 0.9 %select_select_fusion = bf16[1,37,16,3,128]{4,1,3,0,2:T(8,128)(2,1)} fusion(bf16[1,37,16,3,128]{4,1,3,0,2:T(8,128)(2,1)S(1)} %bitcast.36, pred[16,3]{1,0:T(8,128)(4,1)S(1)} %compare_and_fusion, pred[16,3]{1,0:T(8,128)(4,1)S(1)} %broadcast_in_dim.63), kind=kLoop, calls=%fused_computation.10 | loop fusion | flops 454656 | bytes 909408 | tf_op jit(solution)/shard_map/jit(_where)/select_n | solution.py:43
  8.6 7.4 %all-to-all-start = ((bf16[1,37,16,3,128]{4,1,3,0,2:T(8,128)(2,1)}), bf16[1,37,16,3,128]{4,1,3,0,2:T(8,128)(2,1)S(1)}, u32[]{:S(2)}, u32[]{:S(2)}) async-start(bf16[1,37,16,3,128]{4,1,3,0,2:T(8,128)(2,1)} %select_select_fusion), calls=%async_computation | async-start | bytes 983040 | tf_op jit(solution)/shard_map/all_to_all | solution.py:61
  16.1 0.8 %reshape.127 = bf16[1,37,2048]{2,1,0:T(8,128)(2,1)} reshape(bf16[1,37,16,128]{3,2,1,0:T(8,128)(2,1)S(1)} %copy.27) | data formatting | bytes 303104 | tf_op jit(solution)/shard_map/reshape | solution.py:59
  16.8 12.9 %all-to-all-done = bf16[1,37,16,3,128]{4,1,3,0,2:T(8,128)(2,1)S(1)} async-done(((bf16[1,37,16,3,128]{4,1,3,0,2:T(8,128)(2,1)}), bf16[1,37,16,3,128]{4,1,3,0,2:T(8,128)(2,1)S(1)}, u32[]{:S(2)}, u32[]{:S(2)}) %all-to-all-start) | async-done | bytes 454688 | tf_op jit(solution)/shard_map/all_to_all | solution.py:61
  29.8 0.8 %copy.29 = bf16[3,37,16,128]{3,2,1,0:T(8,128)(2,1)} copy(bf16[3,37,16,128]{3,1,0,2:T(8,128)(2,1)S(1)} %bitcast.35) | data formatting | bytes 909312
  (7 shorter events, 0.1 us)
Async XLA Ops:
  4.4 0.8 %copy-start.1 = (f32[16,37,4]{1,2,0:T(4,128)S(1)}, f32[16,37,4]{1,2,0:T(4,128)}, u32[]{:S(2)}) copy-start(f32[16,37,4]{1,2,0:T(4,128)} %param.9) | copy-start | bytes 28420
  4.4 0.9 %copy-start.2 = (s32[16,37]{1,0:T(8,128)S(1)}, s32[16,37]{1,0:T(8,128)}, u32[]{:S(2)}) copy-start(s32[16,37]{1,0:T(8,128)} %param.8) | copy-start | bytes 7108
  4.4 1.0 %copy-start.3 = (s32[2048]{0:T(1024)S(1)}, s32[2048]{0:T(1024)}, u32[]{:S(2)}) copy-start(s32[2048]{0:T(1024)} %param.6) | copy-start | bytes 24580
  4.4 1.1 %copy-start = (bf16[1,137,2048]{2,1,0:T(8,128)(2,1)S(1)}, bf16[1,137,2048]{2,1,0:T(8,128)(2,1)}, u32[]{:S(2)}) copy-start(bf16[1,137,2048]{2,1,0:T(8,128)(2,1)} %param.5) | copy-start | bytes 1683460
  8.6 21.1 %all-to-all-start = ((bf16[1,37,16,3,128]{4,1,3,0,2:T(8,128)(2,1)}), bf16[1,37,16,3,128]{4,1,3,0,2:T(8,128)(2,1)S(1)}, u32[]{:S(2)}, u32[]{:S(2)}) async-start(bf16[1,37,16,3,128]{4,1,3,0,2:T(8,128)(2,1)} %select_select_fusion), calls=%async_computation | async-start | bytes 983040 | tf_op jit(solution)/shard_map/all_to_all | solution.py:61
where the time goes:
time: 30.9 us; the launch traced here: 30.6 us
  waiting for transfers between devices  12.9 us (42%)
  starting transfers between devices  7.39 us (24%)
  local copies, waits for them, and re-layouts  4.66 us (15%)
  other arithmetic  4.52 us (15%)
  between operations  0.76 us (2%)
  matrix products  0.34 us (1%)
    all_to_all x1, waiting for transfers between devices, per_device(): lax.all_to_all(packed, 'col', split_axis=2, concat_axis=0, tiled=True)  12.9 us
    all_to_all x1, starting transfers between devices, per_device(): lax.all_to_all(packed, 'col', split_axis=2, concat_axis=0, tiled=True)  7.39 us
    unnamed x12, local copies, waits for them, and re-layouts  2.94 us
    select_n x1, other arithmetic, pack_slots(): jnp.where(occupied[None, None, :, None], taken, jnp.zeros((), data.dtype))  0.95 us
    reduce_sum x1, other arithmetic, level_matrices(): jnp.sum(weights[:, :, :, None] * hit.astype(jnp.float32), axis=2)  0.9 us
    reduce_sum x1, other arithmetic, slot_tables(): slot = jnp.sum(before * onehot, axis=1)  0.84 us
    reshape x1, local copies, waits for them, and re-layouts, per_device(): timemajor = result.reshape(steps_here, PLEV, blocks * CBLK)  0.76 us
    convert_element_type x1, other arithmetic, slot_tables(): (owner[:, None] == jnp.arange(devices, dtype=jnp.int32)[None, :]).astype(...  0.73 us
  transfers between devices with their start and end apart: 1, of which 1 were waited for; matrix products, arithmetic and copies ran while one was open for 3% of the time, Pallas kernels for 0%

commit v1 on v0

v1 whole, which is shorter than its diff:
```python
import functools

import jax
import jax.numpy as jnp
from jax import lax
from jax.experimental import pallas as pl
from jax.experimental.pallas import tpu as pltpu
from jax.sharding import PartitionSpec as P

LEV = 137
PLEV = 37
BAND = 4
CBLK = 128
MOST = 3
LOW = (LEV // 2 - 1) // 16 * 16
ROWS = -(-MOST * PLEV // 8) * 8
CHUNKS = 4


def loop(count, body):
    if count <= 16:
        for i in range(count):
            body(i)
    else:

        def step(i, carry):
            body(i)
            return carry

        lax.fori_loop(0, count, step, 0)


def partner(me, k, n):
    if n & (n - 1):
        return (me + k) % n
    other = me
    bit = 1
    while bit < n:
        flip = (k // bit) % 2
        other = other + flip * bit * (1 - 2 * ((me // bit) % 2))
        bit *= 2
    return other


def kernel(n, blocks, fields, counts, owner, starts, weights, tm, arrived,
           data, res, stage, packed, table, load_sem, send_sem, recv_sem):
    me = lax.axis_index("col")
    width = data.shape[1] // CHUNKS
    loads = []
    for i in range(CHUNKS):
        span = pl.ds(i * width, width)
        load = pltpu.make_async_copy(fields.at[0, :, span], data.at[:, span], load_sem.at[i])
        load.start()
        loads.append(load)

    barrier = pltpu.get_barrier_semaphore()

    def greet(i):
        pl.semaphore_signal(
            barrier, inc=1, device_id={"col": partner(me, n - 1 - i, n)},
            device_id_type=pl.DeviceIdType.MESH,
        )

    loop(n - 1, greet)

    def find(d):
        seen = jnp.int32(0)
        found = [jnp.int32(blocks)] * MOST

        def look(b, carry):
            seen, found = carry
            hit = owner[b] == d
            found = [jnp.where(hit & (seen == s), b, f) for s, f in enumerate(found)]
            return seen + hit.astype(jnp.int32), found

        if blocks <= 16:
            for b in range(blocks):
                seen, found = look(b, (seen, found))
        else:
            seen, found = lax.fori_loop(0, blocks, look, (seen, found))
        for s in range(MOST):
            table[d * MOST + s] = found[s]

    loop(n, find)

    res[blocks] = jnp.zeros(res.shape[1:], jnp.float32)
    stage[...] = jnp.zeros_like(stage)

    def interpolate(b):
        cols = pl.ds(pl.multiple_of(b * CBLK, CBLK), CBLK)
        count = counts[pl.ds(b, 1), :]
        high = data[LOW:, cols].astype(jnp.float32)
        lev = LOW + lax.broadcasted_iota(jnp.int32, high.shape, 0)
        last = jnp.sum(jnp.where(lev == count - 1, high, 0.0), axis=0, keepdims=True)
        high = jnp.where(lev < count, high, last).astype(jnp.bfloat16)
        filled = jnp.concatenate([data[:LOW, cols], high], axis=0)
        start = starts[pl.ds(b, 1), :]
        offset = lax.broadcasted_iota(jnp.int32, (LEV, PLEV), 0) - start
        matrix = jnp.zeros((LEV, PLEV), jnp.float32)
        for k in range(BAND):
            matrix = jnp.where(offset == k, weights[b, pl.ds(k, 1), :], matrix)
        out = lax.dot_general(
            matrix.astype(jnp.bfloat16), filled, (((0,), (0,)), ((), ())),
            preferred_element_type=jnp.float32,
        )
        res[b, :PLEV] = out
        tm[0, :, cols] = out.astype(jnp.bfloat16)

    per = blocks // CHUNKS
    for i in range(CHUNKS):
        loads[i].wait()
        if blocks <= 16:
            for b in range(i * per, (i + 1) * per):
                interpolate(b)
        else:
            def step(b, carry, i=i):
                interpolate(b + i * per)
                return carry

            lax.fori_loop(0, per, step, 0)

    def pack(d):
        for s in range(MOST):
            stage[s * PLEV:(s + 1) * PLEV] = res[table[d * MOST + s], :PLEV]
        return stage[...].astype(jnp.bfloat16)

    pl.semaphore_wait(barrier, n - 1)

    def copy_to(k):
        d = partner(me, k, n)
        return pltpu.make_async_remote_copy(
            src_ref=packed.at[k], dst_ref=arrived.at[me],
            send_sem=send_sem.at[k], recv_sem=recv_sem.at[me],
            device_id={"col": d}, device_id_type=pl.DeviceIdType.MESH,
        )

    def send(i):
        k = n - 1 - i
        packed[k] = pack(partner(me, k, n))
        copy_to(k).start()

    loop(n - 1, send)
    arrived[me] = pack(me)

    def finish(i):
        k = i + 1
        src = partner(me, k, n) if not (n & (n - 1)) else (me + n - k) % n
        pltpu.make_async_remote_copy(
            src_ref=packed.at[k], dst_ref=arrived.at[src],
            send_sem=send_sem.at[k], recv_sem=recv_sem.at[src],
            device_id={"col": src}, device_id_type=pl.DeviceIdType.MESH,
        ).wait_recv()
        copy_to(k).wait_send()

    loop(n - 1, finish)


def per_device(fields, level_count, owner, band_start, interp_weights):
    n = lax.axis_size("col")
    blocks = owner.shape[0]
    vmem = pl.BlockSpec(memory_space=pltpu.VMEM)
    timemajor, arrived = pl.pallas_call(
        functools.partial(kernel, n, blocks),
        out_shape=(
            jax.ShapeDtypeStruct((1, PLEV, blocks * CBLK), jnp.bfloat16),
            jax.ShapeDtypeStruct((n, ROWS, CBLK), jnp.bfloat16),
        ),
        in_specs=[
            pl.BlockSpec(memory_space=pl.ANY), vmem,
            pl.BlockSpec(memory_space=pltpu.SMEM), vmem, vmem,
        ],
        out_specs=(vmem, vmem),
        scratch_shapes=[
            pltpu.VMEM((LEV, blocks * CBLK), jnp.bfloat16),
            pltpu.VMEM((blocks + 1, -(-PLEV // 8) * 8, CBLK), jnp.float32),
            pltpu.VMEM((ROWS, CBLK), jnp.float32),
            pltpu.VMEM((n, ROWS, CBLK), jnp.bfloat16),
            pltpu.SMEM((n * MOST,), jnp.int32),
            pltpu.SemaphoreType.DMA((CHUNKS,)),
            pltpu.SemaphoreType.DMA((n,)),
            pltpu.SemaphoreType.DMA((n,)),
        ],
        compiler_params=pltpu.CompilerParams(collective_id=0, has_side_effects=True),
    )(
        fields, level_count.reshape(blocks, CBLK), owner, band_start,
        jnp.swapaxes(interp_weights, 1, 2),
    )
    series = arrived[:, :MOST * PLEV].reshape(n, MOST, PLEV, CBLK)
    return (timemajor, jnp.transpose(series, (1, 2, 0, 3)))


def solution(mesh):
    placed = (P(("groups", "col"), None, None), P(), P(), P(), P())
    return jax.shard_map(
        per_device,
        mesh=mesh,
        in_specs=placed,
        out_specs=(P(("groups", "col"), None, None), P(("groups", "col"), None, None, None)),
        check_vma=False,
    )
```

time: 30.9 us -> 22.9 us (0.74)
  Pallas kernels: 0 us -> 19.5 us
  waiting for transfers between devices: 12.9 us -> 0 us
  starting transfers between devices: 7.39 us -> 0 us
  other arithmetic: 4.52 us -> 0 us
  local copies, waits for them, and re-layouts: 4.66 us -> 2.61 us
  matrix products: 0.34 us -> 0 us
    pallas_call x0 -> x1, Pallas kernels: none -> 19.5 us  [per_device(): pl.pallas_call(functools.partial(kernel, n, blocks), out_shape=(jax.Shape...]
    all_to_all x1 -> x0, waiting for transfers between devices: 12.9 us -> none  [per_device(): lax.all_to_all(packed, 'col', split_axis=2, concat_axis=0, tiled=True)]
    all_to_all x1 -> x0, starting transfers between devices: 7.39 us -> none  [per_device(): lax.all_to_all(packed, 'col', split_axis=2, concat_axis=0, tiled=True)]
    unnamed x12 -> x3, local copies, waits for them, and re-layouts: 2.94 us -> 0.67 us
    reduce_sum x4 -> x0, other arithmetic: 2.02 us -> none  [the longest x1 0.9 us: level_matrices(): jnp.sum(weights[:, :, :, None] * hit.astype(jnp.float32), axis=2)]
    slice x0 -> x1, local copies, waits for them, and re-layouts: none -> 1.94 us  [per_device(): series = arrived[:, :MOST * PLEV].reshape(n, MOST, PLEV, CBLK)]
    select_n x2 -> x0, other arithmetic: 0.95 us -> none  [the longest x1 0.95 us: pack_slots(): jnp.where(occupied[None, None, :, None], taken, jnp.zeros((), data.dtype))]
    reshape x2 -> x0, local copies, waits for them, and re-layouts: 0.86 us -> none  [the longest x1 0.76 us: per_device(): timemajor = result.reshape(steps_here, PLEV, blocks * CBLK)]
  transfers between devices with their start and end apart: 1 -> 0, of which waited for: 1 -> 0; matrix products, arithmetic and copies ran while one was open for 3% -> 0% of each run, Pallas kernels for 0% -> 0%
where the time goes in v1:
time: 22.9 us; the launch traced here: 22.7 us
  Pallas kernels  19.5 us (85%)
  local copies, waits for them, and re-layouts  2.61 us (11%)
  between operations  0.65 us (3%)
    pallas_call x1, Pallas kernels, per_device(): pl.pallas_call(functools.partial(kernel, n, blocks), out_shape=(jax.Shape...  19.5 us
    slice x1, local copies, waits for them, and re-layouts, per_device(): series = arrived[:, :MOST * PLEV].reshape(n, MOST, PLEV, CBLK)  1.94 us
    unnamed x3, local copies, waits for them, and re-layouts  0.67 us

profile of v1, /device:TPU:0, one launch (start us, length us, event | category | flops | bytes accessed | tf_op | source)
XLA Modules:
  0.0 22.7 jit_solution(10518820404415534659)
XLA Ops:
  0.6 19.5 %shard_map.68 = (bf16[1,37,2048]{2,1,0:T(8,128)(2,1)}, bf16[16,112,128]{2,1,0:T(8,128)(2,1)}) custom-call(bf16[1,137,2048]{2,1,0:T(8,128)(2,1)} %fields.1, s32[16,128]{1,0:T(8,128)} %bitcast.9, s32[16]{0:T(128)} %owner.1, s32[16,37]{1,0:T(8,128)} %starts.1, f32[16,4,37]{2,1,0:T(4,128)} %bitcast.8), custom_call_target="tpu_custom_call" | custom-call | tf_op jit(solution)/shard_map/pallas_call | solution.py:162
  20.1 0.0 copy-start
  20.1 1.9 %copy.8 = bf16[16,111,128]{2,0,1:T(8,128)(2,1)} copy(bf16[16,111,128]{2,1,0:T(8,128)(2,1)} %bitcast.6) | data formatting | bytes 909312 | tf_op jit(solution)/shard_map/slice | solution.py:188
  22.0 0.0 copy-done
  22.0 0.7 %copy.10 = bf16[1,37,2048]{2,1,0:T(8,128)(2,1)} copy(bf16[1,37,2048]{2,1,0:T(8,128)(2,1)S(1)} %copy-done) | data formatting | bytes 303104
Async XLA Ops:
  20.1 2.0 %copy-start = (bf16[1,37,2048]{2,1,0:T(8,128)(2,1)S(1)}, bf16[1,37,2048]{2,1,0:T(8,128)(2,1)}, u32[]{:S(2)}) copy-start(bf16[1,37,2048]{2,1,0:T(8,128)(2,1)} %get-tuple-element.8) | copy-start | bytes 454660

commit v2 on v1

--- a/solution.py
+++ b/solution.py
@@ -31,8 +31,7 @@
 
 
 def partner(me, k, n):
-    if n & (n - 1):
-        return (me + k) % n
+    return (me + k) % n
     other = me
     bit = 1
     while bit < n:
@@ -42,9 +41,27 @@
     return other
 
 
-def kernel(n, blocks, fields, counts, owner, starts, weights, tm, arrived,
-           data, res, stage, packed, table, load_sem, send_sem, recv_sem):
+def kernel(n, blocks, fields, counts_in, owner_in, starts_in, weights_in, tm_out, arrived,
+           data, counts, owner, starts, weights, tm, res, stage, packed, table,
+           load_sem, small_sem, out_sem, send_sem, recv_sem):
     me = lax.axis_index("col")
+    barrier = pltpu.get_barrier_semaphore()
+
+    def greet(i):
+        pl.semaphore_signal(
+            barrier, inc=1, device_id={"col": partner(me, n - 1 - i, n)},
+            device_id_type=pl.DeviceIdType.MESH,
+        )
+
+    loop(n - 1, greet)
+
+    smalls = []
+    for i, (src, dst) in enumerate(
+        [(owner_in, owner), (counts_in, counts), (starts_in, starts), (weights_in, weights)]
+    ):
+        small = pltpu.make_async_copy(src, dst, small_sem.at[i])
+        small.start()
+        smalls.append(small)
     width = data.shape[1] // CHUNKS
     loads = []
     for i in range(CHUNKS):
@@ -53,15 +70,7 @@
         load.start()
         loads.append(load)
 
-    barrier = pltpu.get_barrier_semaphore()
-
-    def greet(i):
-        pl.semaphore_signal(
-            barrier, inc=1, device_id={"col": partner(me, n - 1 - i, n)},
-            device_id_type=pl.DeviceIdType.MESH,
-        )
-
-    loop(n - 1, greet)
+    smalls[0].wait()
 
     def find(d):
         seen = jnp.int32(0)
@@ -106,6 +115,8 @@
         res[b, :PLEV] = out
         tm[0, :, cols] = out.astype(jnp.bfloat16)
 
+    for small in smalls[1:]:
+        small.wait()
     per = blocks // CHUNKS
     for i in range(CHUNKS):
         loads[i].wait()
@@ -124,7 +135,8 @@
             stage[s * PLEV:(s + 1) * PLEV] = res[table[d * MOST + s], :PLEV]
         return stage[...].astype(jnp.bfloat16)
 
-    pl.semaphore_wait(barrier, n - 1)
+    tm_copy = pltpu.make_async_copy(tm, tm_out, out_sem.at[0])
+    tm_copy.start()
 
     def copy_to(k):
         d = partner(me, k, n)
@@ -134,17 +146,25 @@
             device_id={"col": d}, device_id_type=pl.DeviceIdType.MESH,
         )
 
+    def fill(k):
+        packed[k] = pack(partner(me, k, n))
+
+    loop(n, fill)
+    own = pltpu.make_async_copy(packed.at[0], arrived.at[me], out_sem.at[1])
+    own.start()
+    pl.semaphore_wait(barrier, n - 1)
+
+    def order(i):
+        return i + 1
+
     def send(i):
-        k = n - 1 - i
-        packed[k] = pack(partner(me, k, n))
-        copy_to(k).start()
+        copy_to(order(i)).start()
 
     loop(n - 1, send)
-    arrived[me] = pack(me)
 
     def finish(i):
         k = i + 1
-        src = partner(me, k, n) if not (n & (n - 1)) else (me + n - k) % n
+        src = (me + n - k) % n
         pltpu.make_async_remote_copy(
             src_ref=packed.at[k], dst_ref=arrived.at[src],
             send_sem=send_sem.at[k], recv_sem=recv_sem.at[src],
@@ -153,37 +173,51 @@
         copy_to(k).wait_send()
 
     loop(n - 1, finish)
+    own.wait()
+    tm_copy.wait()
 
 
 def per_device(fields, level_count, owner, band_start, interp_weights):
     n = lax.axis_size("col")
     blocks = owner.shape[0]
-    vmem = pl.BlockSpec(memory_space=pltpu.VMEM)
+    anywhere = pl.BlockSpec(memory_space=pl.ANY)
+    cols = blocks * CBLK
+    tall = -(-PLEV // 8) * 8
+    grant = 2 * cols * (LEV + PLEV + 18) + 4 * CBLK * tall * (blocks + 1) + 2 * n * ROWS * CBLK
+    grant += blocks * 12 * CBLK * 4 + (3 << 20)
     timemajor, arrived = pl.pallas_call(
         functools.partial(kernel, n, blocks),
         out_shape=(
-            jax.ShapeDtypeStruct((1, PLEV, blocks * CBLK), jnp.bfloat16),
+            jax.ShapeDtypeStruct((1, PLEV, cols), jnp.bfloat16),
             jax.ShapeDtypeStruct((n, ROWS, CBLK), jnp.bfloat16),
         ),
-        in_specs=[
-            pl.BlockSpec(memory_space=pl.ANY), vmem,
-            pl.BlockSpec(memory_space=pltpu.SMEM), vmem, vmem,
-        ],
-        out_specs=(vmem, vmem),
+        in_specs=[pl.BlockSpec(memory_space=pltpu.HBM)] * 5,
+        out_specs=(anywhere, anywhere),
         scratch_shapes=[
-            pltpu.VMEM((LEV, blocks * CBLK), jnp.bfloat16),
-            pltpu.VMEM((blocks + 1, -(-PLEV // 8) * 8, CBLK), jnp.float32),
+            pltpu.VMEM((LEV, cols), jnp.bfloat16),
+            pltpu.VMEM((blocks, CBLK), jnp.int32),
+            pltpu.SMEM((blocks,), jnp.int32),
+            pltpu.VMEM((blocks, PLEV), jnp.int32),
+            pltpu.VMEM((blocks, BAND, PLEV), jnp.float32),
+            pltpu.VMEM((1, PLEV, cols), jnp.bfloat16),
+            pltpu.VMEM((blocks + 1, tall, CBLK), jnp.float32),
             pltpu.VMEM((ROWS, CBLK), jnp.float32),
             pltpu.VMEM((n, ROWS, CBLK), jnp.bfloat16),
             pltpu.SMEM((n * MOST,), jnp.int32),
             pltpu.SemaphoreType.DMA((CHUNKS,)),
+            pltpu.SemaphoreType.DMA((4,)),
+            pltpu.SemaphoreType.DMA((2,)),
             pltpu.SemaphoreType.DMA((n,)),
             pltpu.SemaphoreType.DMA((n,)),
         ],
-        compiler_params=pltpu.CompilerParams(collective_id=0, has_side_effects=True),
+        compiler_params=pltpu.CompilerParams(
+            collective_id=0, has_side_effects=True, vmem_limit_bytes=grant
+        ),
     )(
-        fields, level_count.reshape(blocks, CBLK), owner, band_start,
-        jnp.swapaxes(interp_weights, 1, 2),
+        *[pltpu.with_memory_space_constraint(x, pltpu.HBM) for x in (
+            fields, level_count.reshape(blocks, CBLK), owner, band_start,
+            jnp.swapaxes(interp_weights, 1, 2),
+        )]
     )
     series = arrived[:, :MOST * PLEV].reshape(n, MOST, PLEV, CBLK)
     return (timemajor, jnp.transpose(series, (1, 2, 0, 3)))

time: 22.9 us -> 18.5 us (0.81)
  the two profiles are of different devices: /device:TPU:0 before, /device:TPU:9 now
where the time goes in v2:
time: 18.5 us; the launch traced here: 18.4 us
  Pallas kernels  16.2 us (88%)
  local copies, waits for them, and re-layouts  1.55 us (8%)
  between operations  0.64 us (3%)
    pallas_call x1, Pallas kernels, per_device(): pl.pallas_call(functools.partial(kernel, n, blocks), out_shape=(jax.Shape...  16.2 us
    slice x1, local copies, waits for them, and re-layouts, per_device(): series = arrived[:, :MOST * PLEV].reshape(n, MOST, PLEV, CBLK)  0.88 us
    unnamed x1, local copies, waits for them, and re-layouts  0.67 us

profile of v2, /device:TPU:9, one launch (start us, length us, event | category | flops | bytes accessed | tf_op | source)
XLA Modules:
  0.0 18.4 jit_solution(16610380412238689636)
XLA Ops:
  0.6 16.2 %shard_map.68 = (bf16[1,37,2048]{2,1,0:T(8,128)(2,1)S(1)}, bf16[16,112,128]{2,1,0:T(8,128)(2,1)S(1)}) custom-call(bf16[1,137,2048]{2,1,0:T(8,128)(2,1)} %fields.1, s32[16,128]{1,0:T(8,128)} %bitcast.9, s32[16]{0:T(128)} %owner_in.1, s32[16,37]{1,0:T(8,128)} %starts_in.1, f32[16,4,37]{2,1,0:T(4,128)} %bitcast.8), custom_call_target="tpu_custom_call" | custom-call | tf_op jit(solution)/shard_map/pallas_call | solution.py:188
  16.8 0.9 %copy.8 = bf16[16,111,128]{2,0,1:T(8,128)(2,1)} copy(bf16[16,111,128]{2,1,0:T(8,128)(2,1)S(1)} %bitcast.6) | data formatting | bytes 909312 | tf_op jit(solution)/shard_map/slice | solution.py:222
  17.7 0.7 %copy.10 = bf16[1,37,2048]{2,1,0:T(8,128)(2,1)} copy(bf16[1,37,2048]{2,1,0:T(8,128)(2,1)S(1)} %get-tuple-element.8) | data formatting | bytes 303104
